TPU v7x, 64 devices: a 2x2x8 block of a 4x4x8 slice. The times are simulated.
64 devices in a mesh: dp: 4 (over x, y), ep: 16 (over z, core).
Axes of the slice: x: 2, y: 2, z: 8, core: 2. Of those that a mesh axis runs over, the one named last changes fastest.
The devices are a block of a 4x4x8 slice.
Arguments:
- hidden: bfloat16 [16384, 2048], P(('dp', 'ep')), parts along dimension 0
- norm_gain: float32 [2048], replicated
- router_w: bfloat16 [2048, 64], replicated
- topk_idx: int32 [16384, 6], P(('dp', 'ep')), parts along dimension 0
- w_gate: bfloat16 [64, 2048, 1408], P('ep')
- w_up: bfloat16 [64, 2048, 1408], P('ep')
- w_down: bfloat16 [64, 1408, 2048], P('ep')
- shared_gate: bfloat16 [2048, 2816], replicated
- shared_up: bfloat16 [2048, 2816], replicated
- shared_down: bfloat16 [2816, 2048], replicated
Outputs:
- output: bfloat16 [16384, 2048], P(('dp', 'ep')), parts along dimension 0
There are 4 independent parts. A program takes and returns all parts, laid end to end along the dimension named above; an argument that names none is the same for every part.
All inputs are finite; a program needn't handle non-finite values.
Results may differ from a plain program's by a relative error of at most 0.00127.
Values are sent between devices in bfloat16 or wider.
A program may use at most 768 MiB of HBM per device.

v0:
```python
import jax
import jax.numpy as jnp
from jax import lax
from jax.sharding import PartitionSpec as P

NORM_EPS = 1e-6


def rms_norm(hidden, norm_gain):
    hidden_f32 = hidden.astype(jnp.float32)
    inv_rms = lax.rsqrt(jnp.mean(hidden_f32 * hidden_f32, axis=-1, keepdims=True) + NORM_EPS)
    return (hidden_f32 * inv_rms * norm_gain).astype(jnp.bfloat16)


def shared_swiglu(normed, shared_gate, shared_up, shared_down):
    gate_out = jnp.dot(normed, shared_gate, preferred_element_type=jnp.float32)
    up_out = jnp.dot(normed, shared_up, preferred_element_type=jnp.float32)
    activated = (jax.nn.silu(gate_out) * up_out).astype(jnp.bfloat16)
    return jnp.dot(activated, shared_down, preferred_element_type=jnp.float32)


def route_weights(normed, router_w, topk_idx):
    logits = jnp.dot(normed, router_w, preferred_element_type=jnp.float32)
    return jnp.take_along_axis(jax.nn.softmax(logits, axis=-1), topk_idx, axis=1)


def route_layout(topk_idx, num_experts, capacity, group_size):
    tok_count, top_k = topk_idx.shape
    row_count = tok_count * top_k
    local_count = num_experts // group_size
    flat_expert = topk_idx.reshape(-1)
    row_order = jnp.argsort(flat_expert, stable=True)
    sorted_expert = flat_expert[row_order]
    counts = jnp.zeros((num_experts,), jnp.int32).at[flat_expert].add(1)
    rank_sorted = jnp.arange(row_count) - (jnp.cumsum(counts) - counts)[sorted_expert]
    slot_sorted = ((sorted_expert % local_count) * group_size + sorted_expert // local_count) * capacity + rank_sorted
    row_slot = jnp.zeros((row_count,), jnp.int32).at[row_order].set(slot_sorted)
    slot_token = jnp.full((num_experts * capacity,), tok_count, jnp.int32).at[slot_sorted].set(row_order // top_k)
    return row_slot, slot_token


def expert_swiglu(expert_in, w_gate, w_up, w_down):
    gate_out = jnp.einsum('ech,ehi->eci', expert_in, w_gate, preferred_element_type=jnp.float32)
    up_out = jnp.einsum('ech,ehi->eci', expert_in, w_up, preferred_element_type=jnp.float32)
    activated = (jax.nn.silu(gate_out) * up_out).astype(jnp.bfloat16)
    return jnp.einsum('eci,eih->ech', activated, w_down, preferred_element_type=jnp.float32).astype(jnp.bfloat16)


def finish_output(hidden, shared_out, row_out, route_w):
    routed = jnp.sum(row_out.astype(jnp.float32) * route_w[:, :, None], axis=1)
    return (hidden.astype(jnp.float32) + shared_out + routed).astype(jnp.bfloat16)


def solution(mesh):
    group_size = mesh.shape['ep']

    def local_step(hidden, norm_gain, router_w, topk_idx, w_gate, w_up, w_down, shared_gate, shared_up, shared_down):
        tok_count, hidden_size = hidden.shape
        top_k = topk_idx.shape[1]
        num_experts = router_w.shape[1]
        local_count = w_gate.shape[0]
        capacity = 3 * tok_count * top_k // (2 * num_experts)
        normed = rms_norm(hidden, norm_gain)
        route_w = route_weights(normed, router_w, topk_idx)
        row_slot, slot_token = route_layout(topk_idx, num_experts, capacity, group_size)
        normed_pad = jnp.concatenate([normed, jnp.zeros((1, hidden_size), normed.dtype)], axis=0)
        send_buf = normed_pad[slot_token].reshape(local_count, group_size, capacity, hidden_size)
        recv_buf = lax.all_to_all(send_buf, 'ep', 1, 1, tiled=True)
        expert_out = expert_swiglu(recv_buf.reshape(local_count, group_size * capacity, hidden_size), w_gate, w_up, w_down)
        back_buf = lax.all_to_all(expert_out.reshape(local_count, group_size, capacity, hidden_size), 'ep', 1, 1, tiled=True)
        shared_out = shared_swiglu(normed, shared_gate, shared_up, shared_down)
        row_out = back_buf.reshape(local_count * group_size * capacity, hidden_size)[row_slot]
        return finish_output(hidden, shared_out, row_out.reshape(tok_count, top_k, hidden_size), route_w)

    token_spec = P(('dp', 'ep'), None)
    expert_spec = P('ep', None, None)
    return jax.shard_map(
        local_step,
        mesh=mesh,
        in_specs=(token_spec, P(None), P(None, None), token_spec, expert_spec, expert_spec, expert_spec,
                  P(None, None), P(None, None), P(None, None)),
        out_specs=token_spec,
        check_vma=False,
    )
```

profile of v0, /device:TPU:21, one launch (start us, length us, event | category | flops | bytes accessed | tf_op | source)
XLA Modules:
  0.0 771.2 jit_solution(12185931775795024836)
XLA Ops:
  0.0 0.9 copy.38
  1.3 11.1 %scatter_custom_fusion = s32[64]{0:T(128)S(1)} fusion(s32[1536]{0:T(1024)S(1)} %fusion.21, s32[1536]{0:T(1024)S(1)} %broadcast.325, s32[]{:T(128)} %constant.72.clone.1), kind=kCustom, calls=%fused_computation.135 | custom fusion | flops 1536 | bytes 260 | tf_op jit(solution)/shard_map/scatter-add | solution.py:34
  12.7 0.7 fusion.35
  13.4 0.7 fusion.32
  14.1 0.7 fusion.33
  14.9 0.7 fusion.34
  15.6 5.0 sort.17
  21.3 8.4 %gather_fusion = s32[1536]{0:T(1024)S(1)} fusion(s32[1536]{0:T(1024)S(1)} %reshape.206, s32[2048]{0:T(1024)S(1)} %pad_clamp_fusion.2), kind=kCustom, calls=%fused_computation | custom fusion | bytes 18432 | tf_op jit(solution)/shard_map/gather | solution.py:33
  29.6 4.4 fusion.20
  34.0 1.1 compare_reduce_fusion.56
  35.2 36.2 %fusion.14 = (s32[1536]{0:T(1024)}, s32[1536]{0:T(1024)S(1)}) fusion(s32[1536]{0:T(1024)S(1)} %gather_fusion, pred[1536]{0:T(1024)(128)(4,1)S(1)} %get-tuple-element.63, pred[1536]{0:T(1024)(128)(4,1)S(1)} %get-tuple-element.62, pred[1536]{0:T(1024)(128)(4,1)S(1)} %get-tuple-element.61, pred[1536]{0:T(1024)(128)(4,1)S(1)} %get-tuple-element.60, ...), kind=kLoop, calls=%fused_computation.111 | loop fusion | flops 124416 | bytes 112356 | tf_op jit(solution)/shard_map/add | solution.py:36
  71.5 6.2 scatter_custom_fusion.1
  78.3 1.0 copy-done.1
  79.4 9.9 %gather_fusion.1 = bf16[2304,2048]{1,0:T(8,128)(2,1)} fusion(bf16[257,2048]{1,0:T(8,128)(2,1)S(1)} %concatenate.3, s32[3072]{0:T(1024)S(1)} %pad_clamp_fusion), kind=kCustom, calls=%fused_computation.1 | custom fusion | bytes 18883584 | tf_op jit(solution)/shard_map/gather | solution.py:67
  89.3 13.1 %reshape.210 = bf16[4,16,36,2048]{3,2,1,0:T(8,128)(2,1)} reshape(bf16[2304,2048]{1,0:T(8,128)(2,1)} %gather_fusion.1) | data formatting | bytes 18874368 | tf_op jit(solution)/shard_map/reshape | solution.py:67
  102.3 11.3 %copy.41 = bf16[4,16,36,2048]{3,0,2,1:T(4,128)(2,1)S(1)} copy(bf16[4,16,36,2048]{3,2,1,0:T(8,128)(2,1)} %reshape.210) | data formatting | bytes 18874368 | tf_op jit(solution)/shard_map/reshape | solution.py:67
  113.6 218.5 %all_to_all.10 = bf16[4,16,36,2048]{3,0,2,1:T(4,128)(2,1)} all-to-all(bf16[4,16,36,2048]{3,0,2,1:T(4,128)(2,1)S(1)} %copy.41), channel_id=1, replica_groups=mesh['dp'=4,'ep'=16] {'ep'}, dimensions={1} | all-to-all | bytes 18874368 | tf_op jit(solution)/shard_map/all_to_all | solution.py:68
  332.1 59.2 %fusion.1 = f32[4,576,1408]{2,1,0:T(8,128)} fusion(bf16[4,2048,1408]{2,1,0:T(8,128)(2,1)} %param.14, bf16[4,576,2048]{2,0,1:T(4,128)(2,1)} %bitcast.95), kind=kOutput, calls=%fused_computation.10 | convolution fusion | flops 13287555072 | bytes 45481984 | tf_op jit(solution)/shard_map/ech,ehi->eci/dot_general | solution.py:43
  391.3 36.2 %fusion.66 = bf16[4,576,1408]{2,1,0:T(8,128)(2,1)} fusion(bf16[4,2048,1408]{2,1,0:T(8,128)(2,1)} %param.15, bf16[4,576,2048]{2,0,1:T(4,128)(2,1)} %bitcast.96, f32[4,576,1408]{2,1,0:T(8,128)} %fusion.1), kind=kOutput, calls=%bitcast_fusion.clone.1 | convolution fusion | flops 13307019264 | bytes 51970048 | tf_op jit(solution)/shard_map/ech,ehi->eci/dot_general | solution.py:44
  427.6 19.8 %convolution_convert_fusion = bf16[4,576,2048]{2,1,0:T(8,128)(2,1)S(1)} fusion(bf16[4,1408,2048]{2,1,0:T(8,128)(2,1)} %param.16, bf16[4,576,1408]{2,1,0:T(8,128)(2,1)} %fusion.66), kind=kOutput, calls=%fused_computation.12 | convolution fusion | flops 13292273664 | bytes 38993920 | tf_op jit(solution)/shard_map/eci,eih->ech/dot_general | solution.py:46
  447.4 22.9 %copy.44 = bf16[4,576,2048]{2,0,1:T(4,128)(2,1)} copy(bf16[4,576,2048]{2,1,0:T(8,128)(2,1)S(1)} %convolution_convert_fusion) | data formatting | bytes 18874368 | tf_op jit(solution)/shard_map/convert_element_type | solution.py:46
  470.3 5.0 all-to-all-start.1
  475.3 6.3 scatter_custom_fusion.2
  482.5 12.9 %gather_fusion.3 = f32[1536]{0:T(1024)S(1)} fusion(f32[256,64]{0,1:T(8,128)S(1)} %fusion.9, s32[1536]{0:T(1024)S(1)} %reshape.311), kind=kCustom, calls=%fused_computation.3 | custom fusion | bytes 24576 | tf_op jit(solution)/shard_map/jit(take_along_axis)/gather | solution.py:24
  495.9 9.0 %fusion.37 = f32[256,2816]{1,0:T(8,128)} fusion(bf16[256,2048]{1,0:T(8,128)(2,1)S(1)} %copy-done.2, bf16[2048,2816]{1,0:T(8,128)(2,1)} %param.17), kind=kOutput, calls=%fused_computation.143 | convolution fusion | flops 2952790016 | bytes 15466496 | tf_op jit(solution)/shard_map/dot_general | solution.py:16
  504.9 183.2 %all-to-all-done.1 = bf16[4,16,36,2048]{3,0,2,1:T(4,128)(2,1)} async-done(((bf16[4,16,36,2048]{3,0,2,1:T(4,128)(2,1)}), bf16[4,16,36,2048]{3,0,2,1:T(4,128)(2,1)}, u32[]{:S(2)}, u32[]{:S(2)}) %all-to-all-start.1) | async-done | bytes 9437216 | tf_op jit(solution)/shard_map/all_to_all | solution.py:70
  688.2 12.9 %copy.45 = bf16[4,16,36,2048]{3,2,1,0:T(8,128)(2,1)} copy(bf16[4,16,36,2048]{3,0,2,1:T(4,128)(2,1)} %all-to-all-done.1) | data formatting | bytes 18874368 | tf_op jit(solution)/shard_map/all_to_all | solution.py:70
  701.0 13.2 %reshape.213 = bf16[2304,2048]{1,0:T(8,128)(2,1)} reshape(bf16[4,16,36,2048]{3,2,1,0:T(8,128)(2,1)} %copy.45) | data formatting | bytes 18874368 | tf_op jit(solution)/shard_map/reshape | solution.py:72
  714.2 17.9 %gather_fusion.2 = bf16[1536,2048]{1,0:T(8,128)(2,1)} fusion(bf16[2304,2048]{1,0:T(8,128)(2,1)} %reshape.213, s32[2048]{0:T(1024)S(1)} %pad_clamp_fusion.1), kind=kCustom, calls=%fused_computation.2 | custom fusion | bytes 12589056 | tf_op jit(solution)/shard_map/gather | solution.py:72
  732.1 11.7 %reshape.215 = f32[256,6,2048]{2,1,0:T(8,128)} reshape(bf16[1536,2048]{1,0:T(8,128)(2,1)} %gather_fusion.2) | data formatting | bytes 18874368 | tf_op jit(solution)/shard_map/convert_element_type | solution.py:50
  743.8 10.6 %multiply_reduce_fusion = f32[256,2048]{1,0:T(8,128)} fusion(f32[256,6,2048]{2,1,0:T(8,128)} %reshape.215, f32[256,6]{1,0:T(8,128)S(1)} %copy.48), kind=kLoop, calls=%fused_computation.7 | loop fusion | flops 5767168 | bytes 14686208 | tf_op jit(solution)/shard_map/reduce_sum | solution.py:50
  754.5 16.3 %fusion.5 = bf16[256,2048]{1,0:T(8,128)(2,1)} fusion(f32[256,2048]{1,0:T(8,128)} %multiply_reduce_fusion, bf16[2816,2048]{1,0:T(8,128)(2,1)} %param.19, bf16[256,2048]{1,0:T(8,128)(2,1)S(1)} %copy-done.4, bf16[256,2048]{1,0:T(8,128)(2,1)S(1)} %copy-done.2, bf16[2048,2816]{1,0:T(8,128)(2,1)} %param.18, f32[256,2816]{1,0:T(8,128)} %fusion.37), kind=kOutput, calls=%fused_computation.19 | convolution fusion | flops 5912002560 | bytes 31195136 | tf_op jit(solution)/shard_map/dot_general | solution.py:19
  (45 shorter events, 3.2 us)
Async XLA Ops:
  0.0 482.0 %copy-start = (bf16[2048,64]{0,1:T(8,128)(2,1)S(1)}, bf16[2048,64]{0,1:T(8,128)(2,1)}, u32[]{:S(2)}) copy-start(bf16[2048,64]{0,1:T(8,128)(2,1)} %param.12) | copy-start | bytes 786436
  0.0 77.7 %copy-start.3 = (bf16[256,2048]{1,0:T(8,128)(2,1)S(1)}, bf16[256,2048]{1,0:T(8,128)(2,1)}, u32[]{:S(2)}) copy-start(bf16[256,2048]{1,0:T(8,128)(2,1)} %param.10) | copy-start | bytes 3145732
  0.0 78.0 %copy-start.7 = (f32[2048]{0:T(1024)S(1)}, f32[2048]{0:T(1024)}, u32[]{:S(2)}) copy-start(f32[2048]{0:T(1024)} %param.11) | copy-start | bytes 24580
  20.7 0.6 copy-start.6
  78.3 1.0 copy-start.1
  470.3 11.4 %copy-start.5 = (s32[256,6]{0,1:T(8,128)S(1)}, s32[256,6]{0,1:T(8,128)}, u32[]{:S(2)}) copy-start(s32[256,6]{0,1:T(8,128)} %param.13) | copy-start | bytes 18436
  470.3 11.7 %copy-start.2 = (bf16[256,2048]{1,0:T(8,128)(2,1)S(1)}, bf16[256,2048]{1,0:T(8,128)(2,1)}, u32[]{:S(2)}) copy-start(bf16[256,2048]{1,0:T(8,128)(2,1)} %copy-done.1) | copy-start | bytes 3145732
  470.3 217.8 %all-to-all-start.1 = ((bf16[4,16,36,2048]{3,0,2,1:T(4,128)(2,1)}), bf16[4,16,36,2048]{3,0,2,1:T(4,128)(2,1)}, u32[]{:S(2)}, u32[]{:S(2)}) async-start(bf16[4,16,36,2048]{3,0,2,1:T(4,128)(2,1)} %bitcast.94), calls=%async_computation.1 | async-start | bytes 18874368 | tf_op jit(solution)/shard_map/all_to_all | solution.py:70
  743.8 10.6 %copy-start.4 = (bf16[256,2048]{1,0:T(8,128)(2,1)S(1)}, bf16[256,2048]{1,0:T(8,128)(2,1)}, u32[]{:S(2)}) copy-start(bf16[256,2048]{1,0:T(8,128)(2,1)} %param.10) | copy-start | bytes 3145732
where the time goes:
time: 780 us; the launch traced here: 771 us
  blocking collectives  219 us (28%)
  waiting for transfers between devices  183 us (23%)
  local copies, waits for them, and re-layouts  153 us (20%)
  matrix products  141 us (18%)
  other arithmetic  69.6 us (9%)
    all_to_all x1, blocking collectives, local_step(): recv_buf = lax.all_to_all(send_buf, 'ep', 1, 1, tiled=True)  219 us
    all_to_all x1, waiting for transfers between devices, local_step(): lax.all_to_all(expert_out.reshape(local_count, group_size, capacity, hidd...  183 us
    dot_general x1, matrix products, expert_swiglu(): jnp.einsum('ech,ehi->eci', expert_in, w_gate, preferred_element_type=jnp....  59.2 us
    add x1, other arithmetic, route_layout(): (sorted_expert % local_count * group_size + sorted_expert // local_count)...  36.2 us
    dot_general x1, matrix products, expert_swiglu(): jnp.einsum('ech,ehi->eci', expert_in, w_up, preferred_element_type=jnp.fl...  36.2 us
    reshape x2, local copies, waits for them, and re-layouts, local_step(): normed_pad[slot_token]  24.4 us
    convert_element_type x1, local copies, waits for them, and re-layouts, expert_swiglu(): jnp.einsum('eci,eih->ech', activated, w_down, preferred_element_type=jnp....  22.9 us
    dot_general x1, matrix products, expert_swiglu(): jnp.einsum('eci,eih->ech', activated, w_down, preferred_element_type=jnp....  19.8 us
  transfers between devices with their start and end apart: 1, of which 1 were waited for; matrix products, arithmetic and copies ran while one was open for 4% of the time, Pallas kernels for 0%

commit v1 on v0

v1 whole, which is shorter than its diff:
```python
import functools

import jax
import jax.numpy as jnp
from jax import lax
from jax.experimental import pallas as pl
from jax.experimental.pallas import tpu as pltpu
from jax.sharding import PartitionSpec as P

NORM_EPS = 1e-6
QUAD = 4


def rms_norm(hidden, norm_gain):
    hidden_f32 = hidden.astype(jnp.float32)
    inv_rms = lax.rsqrt(jnp.mean(hidden_f32 * hidden_f32, axis=-1, keepdims=True) + NORM_EPS)
    return (hidden_f32 * inv_rms * norm_gain).astype(jnp.bfloat16)


def shared_swiglu(normed, shared_gate, shared_up, shared_down):
    gate_out = jnp.dot(normed, shared_gate, preferred_element_type=jnp.float32)
    up_out = jnp.dot(normed, shared_up, preferred_element_type=jnp.float32)
    activated = (jax.nn.silu(gate_out) * up_out).astype(jnp.bfloat16)
    return jnp.dot(activated, shared_down, preferred_element_type=jnp.float32)


def dense_weights(normed, router_w, topk_idx):
    logits = jnp.dot(normed, router_w, preferred_element_type=jnp.float32)
    probs = jax.nn.softmax(logits, axis=-1)
    experts = lax.broadcasted_iota(jnp.int32, (1, router_w.shape[1], 1), 1)
    chosen = jnp.any(topk_idx[:, None, :] == experts, axis=2)
    return jnp.where(chosen, probs, -1.0).T


def dispatch_kernel(slot_ref, rows_ref, out_ref, pick_ref):
    local_count, block_rows, hidden_size = out_ref.shape
    tokens = rows_ref.shape[0]
    row_id = lax.broadcasted_iota(jnp.int32, (block_rows, tokens), 0)
    for e in range(local_count):
        hit = row_id == slot_ref[0, e:e + 1, :]
        pick_ref[e * block_rows:(e + 1) * block_rows, :] = hit.astype(jnp.float32).astype(jnp.bfloat16)
    step = 512
    for n in range(0, hidden_size, step):
        got = jnp.dot(pick_ref[...], rows_ref[:, n:n + step], preferred_element_type=jnp.float32)
        got = got.astype(jnp.bfloat16)
        for e in range(local_count):
            out_ref[e, :, n:n + step] = got[e * block_rows:(e + 1) * block_rows]


def expert_kernel(x_ref, gate_ref, up_ref, down_ref, out_ref):
    x = x_ref[0]
    gate_out = jnp.dot(x, gate_ref[0], preferred_element_type=jnp.float32)
    up_out = jnp.dot(x, up_ref[0], preferred_element_type=jnp.float32)
    act = (jax.nn.silu(gate_out) * up_out).astype(jnp.bfloat16)
    out_ref[0] = jnp.dot(act, down_ref[0], preferred_element_type=jnp.float32).astype(jnp.bfloat16)


def combine_kernel(capacity, window, rank_ref, weight_ref, rows_ref, out_ref):
    local_count = rank_ref.shape[1]
    tokens, hidden_size = out_ref.shape[1:]
    place = lax.rem(pl.program_id(0), QUAD)
    shift = place * (capacity % 16)
    start = pl.multiple_of(place * (capacity - capacity % 16), 16)
    row_id = lax.broadcasted_iota(jnp.int32, (window, tokens), 0)
    parts = []
    rows = []
    for e in range(local_count):
        slot = rank_ref[0, e:e + 1, :]
        hit = (row_id == slot + shift) & (slot >= 0)
        parts.append(jnp.where(hit, weight_ref[0, e:e + 1, :], 0.0))
        rows.append(rows_ref[e, pl.ds(start, window), :])
    weight = jnp.concatenate(parts, axis=0)
    high = weight.astype(jnp.bfloat16)
    rest = weight - high.astype(jnp.float32)
    mid = rest.astype(jnp.bfloat16)
    low = (rest - mid.astype(jnp.float32)).astype(jnp.bfloat16)
    terms = jnp.concatenate([high, mid, low], axis=0).T
    rows = jnp.concatenate(rows * 3, axis=0)
    step = 512
    for n in range(0, hidden_size, step):
        out_ref[0, :, n:n + step] = jnp.dot(terms, rows[:, n:n + step], preferred_element_type=jnp.float32)


def solution(mesh):
    group_size = mesh.shape['ep']

    def local_step(hidden, norm_gain, router_w, topk_idx, w_gate, w_up, w_down, shared_gate, shared_up, shared_down):
        tok_count, hidden_size = hidden.shape
        top_k = topk_idx.shape[1]
        num_experts = router_w.shape[1]
        local_count, _, ff = w_gate.shape
        capacity = 3 * tok_count * top_k // (2 * num_experts)
        window = 48
        quads = group_size // QUAD
        block_rows = QUAD * capacity
        normed = rms_norm(hidden, norm_gain)
        weight_t = dense_weights(normed, router_w, topk_idx)
        all_weight = lax.all_gather(weight_t, 'ep', axis=0).reshape(group_size, group_size, local_count, tok_count)
        all_rows = lax.all_gather(normed, 'ep', axis=0, tiled=True)
        weight = lax.dynamic_index_in_dim(all_weight, lax.axis_index('ep'), 1, keepdims=False)
        chosen = weight >= 0
        before = jnp.triu(jnp.ones((tok_count, tok_count), jnp.bfloat16), 1)
        rank = jnp.einsum('set,tu->seu', chosen.astype(jnp.bfloat16), before, preferred_element_type=jnp.float32)
        rank = jnp.where(chosen, rank.astype(jnp.int32), -1)
        offset = (jnp.arange(group_size, dtype=jnp.int32) % QUAD * capacity)[:, None, None]
        slot = jnp.where(chosen, rank + offset, -1).reshape(quads, QUAD, local_count, tok_count)
        slot = slot.swapaxes(1, 2).reshape(quads, local_count, QUAD * tok_count)
        params = pltpu.CompilerParams(vmem_limit_bytes=60 * 1024 * 1024)
        expert_in = pl.pallas_call(
            dispatch_kernel,
            grid=(quads,),
            in_specs=[pl.BlockSpec((1, local_count, QUAD * tok_count), lambda q: (q, 0, 0)),
                      pl.BlockSpec((QUAD * tok_count, hidden_size), lambda q: (q, 0))],
            out_specs=pl.BlockSpec((local_count, block_rows, hidden_size), lambda q: (0, q, 0)),
            out_shape=jax.ShapeDtypeStruct((local_count, quads * block_rows, hidden_size), jnp.bfloat16),
            scratch_shapes=[pltpu.VMEM((local_count * block_rows, QUAD * tok_count), jnp.bfloat16)],
            compiler_params=params,
            name='dispatch',
        )(slot, all_rows)
        total_rows = quads * block_rows
        expert_out = pl.pallas_call(
            expert_kernel,
            grid=(local_count,),
            in_specs=[pl.BlockSpec((1, total_rows, hidden_size), lambda e: (e, 0, 0)),
                      pl.BlockSpec((1, hidden_size, ff), lambda e: (e, 0, 0)),
                      pl.BlockSpec((1, hidden_size, ff), lambda e: (e, 0, 0)),
                      pl.BlockSpec((1, ff, hidden_size), lambda e: (e, 0, 0))],
            out_specs=pl.BlockSpec((1, total_rows, hidden_size), lambda e: (e, 0, 0)),
            out_shape=jax.ShapeDtypeStruct((local_count, total_rows, hidden_size), jnp.bfloat16),
            compiler_params=params,
            name='experts',
        )(expert_in, w_gate, w_up, w_down)
        partial = pl.pallas_call(
            functools.partial(combine_kernel, capacity, window),
            grid=(group_size,),
            in_specs=[pl.BlockSpec((1, local_count, tok_count), lambda s: (s, 0, 0)),
                      pl.BlockSpec((1, local_count, tok_count), lambda s: (s, 0, 0)),
                      pl.BlockSpec((local_count, block_rows, hidden_size), lambda s: (0, s // QUAD, 0))],
            out_specs=pl.BlockSpec((1, tok_count, hidden_size), lambda s: (s, 0, 0)),
            out_shape=jax.ShapeDtypeStruct((group_size, tok_count, hidden_size), jnp.float32),
            compiler_params=params,
            name='combine',
        )(rank, weight, expert_out)
        routed = lax.psum_scatter(partial, 'ep', scatter_dimension=0, tiled=False)
        shared_out = shared_swiglu(normed, shared_gate, shared_up, shared_down)
        return (hidden.astype(jnp.float32) + shared_out + routed).astype(jnp.bfloat16)

    token_spec = P(('dp', 'ep'), None)
    expert_spec = P('ep', None, None)
    return jax.shard_map(
        local_step,
        mesh=mesh,
        in_specs=(token_spec, P(None), P(None, None), token_spec, expert_spec, expert_spec, expert_spec,
                  P(None, None), P(None, None), P(None, None)),
        out_specs=token_spec,
        check_vma=False,
    )
```

time: 780 us -> 441 us (0.57); the launches traced: 771 us -> 441 us
  blocking collectives: 219 us -> 0 us
  local copies, waits for them, and re-layouts: 153 us -> 2.71 us
  matrix products: 141 us -> 25.9 us
  waiting for transfers between devices: 183 us -> 298 us
  Pallas kernels: 0 us -> 94.3 us
  other arithmetic: 69.6 us -> 5.91 us
  between operations: 0.75 us -> 13.2 us
    all_to_all x1 -> x0, blocking collectives: 219 us -> none  [local_step(): recv_buf = lax.all_to_all(send_buf, 'ep', 1, 1, tiled=True)]
    all_to_all x1 -> x0, waiting for transfers between devices: 183 us -> none  [local_step(): lax.all_to_all(expert_out.reshape(local_count, group_size, capacity, hidd...]
    reduce_scatter x0 -> x1, waiting for transfers between devices: none -> 169 us  [local_step(): routed = lax.psum_scatter(partial, 'ep', scatter_dimension=0, tiled=False)]
    all_gather x0 -> x2, waiting for transfers between devices: none -> 129 us  [the longest x1 89.1 us: local_step(): all_rows = lax.all_gather(normed, 'ep', axis=0, tiled=True)]
    dot_general x4 -> x2, matrix products: 116 us -> 0.61 us  [the longest x1 0.46 us: dense_weights(): logits = jnp.dot(normed, router_w, preferred_element_type=jnp.float32)]
    pallas_call x0 -> x3, Pallas kernels: none -> 94.3 us  [the longest x1 52.7 us: local_step(): pl.pallas_call(expert_kernel, grid=(local_count,), in_specs=[pl.BlockSpec...]
    gather x12 -> x0, local copies, waits for them, and re-layouts: 52.4 us -> none  [the longest x1 17.9 us: local_step(): back_buf.reshape(local_count * group_size * capacity, hidden_size)[row_slot]]
    reshape x5 -> x1, local copies, waits for them, and re-layouts: 37.8 us -> 1.53 us  [local_step(): lax.all_gather(weight_t, 'ep', axis=0)]
  transfers between devices with their start and end apart: 1 -> 3, of which waited for: 1 -> 3; matrix products, arithmetic and copies ran while one was open for 4% -> 3% of each run, Pallas kernels for 0% -> 0%
where the time goes in v1:
time: 441 us
  waiting for transfers between devices  298 us (68%)
  Pallas kernels  94.3 us (21%)
  matrix products  25.9 us (6%)
  between operations  13.2 us (3%)
  other arithmetic  5.91 us (1%)
    reduce_scatter x1, waiting for transfers between devices, local_step(): routed = lax.psum_scatter(partial, 'ep', scatter_dimension=0, tiled=False)  169 us
    all_gather x1, waiting for transfers between devices, local_step(): all_rows = lax.all_gather(normed, 'ep', axis=0, tiled=True)  89.1 us
    pallas_call x1, Pallas kernels, local_step(): pl.pallas_call(expert_kernel, grid=(local_count,), in_specs=[pl.BlockSpec...  52.7 us
    all_gather x1, waiting for transfers between devices, local_step(): lax.all_gather(weight_t, 'ep', axis=0)  39.5 us
    pallas_call x1, Pallas kernels, local_step(): pl.pallas_call(functools.partial(combine_kernel, capacity, window), grid=...  27 us
    dot_general x1, matrix products, shared_swiglu(): return jnp.dot(activated, shared_down, preferred_element_type=jnp.float32)  16.2 us
    pallas_call x1, Pallas kernels, local_step(): pl.pallas_call(dispatch_kernel, grid=(quads,), in_specs=[pl.BlockSpec((1,...  14.7 us
    dot_general x1, matrix products, shared_swiglu(): gate_out = jnp.dot(normed, shared_gate, preferred_element_type=jnp.float32)  9.06 us
  transfers between devices with their start and end apart: 3, of which 3 were waited for; matrix products, arithmetic and copies ran while one was open for 3% of the time, Pallas kernels for 0%

profile of v1, /device:TPU:21, one launch (start us, length us, event | category | flops | bytes accessed | tf_op | source)
XLA Modules:
  0.0 440.6 jit_solution(7679742563106719203)
XLA Ops:
  6.5 0.0 copy-start
  6.6 0.0 all-gather.6.cloned.1.call-start
  6.6 1.6 fusion.3
  8.1 0.8 fusion.6
  8.9 1.5 fusion.5
  10.4 0.0 copy-start.2
  10.4 0.0 copy-done
  10.4 0.5 fusion.20
  10.9 0.6 select_bitcast_fusion
  11.6 0.1 all-gather.6.cloned.1.call-update
  11.6 0.1 all-gather.4.cloned.1.call-start
  11.7 0.0 copy-done.2
  11.7 0.7 all-gather.4.cloned.1.call-update
  12.5 0.1 reduce-scatter.2.cloned.1.call-start
  12.5 39.5 %all-gather.6.cloned.1.call-done = f32[1024,256]{1,0:T(8,128)} async-done(((f32[64,256]{1,0:T(8,128)}), f32[1024,256]{1,0:T(8,128)}) %all-gather.6.cloned.1.call-update) | async-done | bytes 1048592 | tf_op jit(solution)/shard_map/all_gather | solution.py:98
  52.1 1.5 reshape.31
  53.6 0.6 broadcast_compare_fusion
  54.3 0.1 fusion.9
  54.4 0.7 add_select_fusion
  55.1 89.1 %all-gather.4.cloned.1.call-done.rows_ref = bf16[4096,2048]{1,0:T(8,128)(2,1)} async-done(((bf16[256,2048]{1,0:T(8,128)(2,1)}), bf16[4096,2048]{1,0:T(8,128)(2,1)}) %all-gather.4.cloned.1.call-update) | async-done | bytes 16777232 | tf_op jit(solution)/shard_map/all_gather | solution.py:99
  144.2 14.7 %dispatch.1.x_ref = bf16[4,576,2048]{2,1,0:T(8,128)(2,1)} custom-call(s32[4,4,1024]{2,1,0:T(4,128)} %bitcast.24, bf16[4096,2048]{1,0:T(8,128)(2,1)} %all-gather.4.cloned.1.call-done.rows_ref), custom_call_target="tpu_custom_call" | custom-call | tf_op jit(solution)/shard_map/dispatch/pallas_call | solution.py:109
  158.9 52.7 %experts.1.rows_ref = bf16[4,576,2048]{2,1,0:T(8,128)(2,1)} custom-call(bf16[4,576,2048]{2,1,0:T(8,128)(2,1)} %dispatch.1.x_ref, bf16[4,2048,1408]{2,1,0:T(8,128)(2,1)} %gate_ref.1, bf16[4,2048,1408]{2,1,0:T(8,128)(2,1)} %up_ref.1, bf16[4,1408,2048]{2,1,0:T(8,128)(2,1)} %down_ref.1), custom_call_target="tpu_custom_call" | custom-call | tf_op jit(solution)/shard_map/experts/pallas_call | solution.py:121
  211.6 27.0 %combine.1 = f32[16,256,2048]{2,1,0:T(8,128)} custom-call(s32[16,4,256]{2,1,0:T(4,128)} %get-tuple-element.8.rank_ref, f32[16,4,256]{2,1,0:T(4,128)} %get-tuple-element.6.weight_ref, bf16[4,576,2048]{2,1,0:T(8,128)(2,1)} %experts.1.rows_ref), custom_call_target="tpu_custom_call" | custom-call | tf_op jit(solution)/shard_map/combine/pallas_call | solution.py:133
  238.6 0.0 copy-start.3
  238.6 0.1 reduce-scatter.2.cloned.1.call-update
  238.6 1.2 copy-done.3
  239.8 0.0 copy-start.4
  239.8 9.1 %fusion.21 = f32[256,2816]{1,0:T(8,128)} fusion(bf16[256,2048]{1,0:T(8,128)(2,1)S(1)} %copy-done.3, bf16[2048,2816]{1,0:T(8,128)(2,1)} %param.17), kind=kOutput, calls=%fused_computation.34 | convolution fusion | flops 2952790016 | bytes 15466496 | tf_op jit(solution)/shard_map/dot_general | solution.py:21
  248.8 169.0 %reduce-scatter.2.cloned.1.call-done = f32[1,256,2048]{2,1,0:T(8,128)} async-done(((f32[16,256,2048]{2,1,0:T(8,128)}), f32[1,256,2048]{2,1,0:T(8,128)}) %reduce-scatter.2.cloned.1.call-update) | async-done | bytes 2097168 | tf_op jit(solution)/shard_map/reduce_scatter | solution.py:144
  417.9 0.0 copy-done.4
  417.9 16.2 %fusion.2 = bf16[256,2048]{1,0:T(8,128)(2,1)} fusion(bf16[2816,2048]{1,0:T(8,128)(2,1)} %param.19, bf16[256,2048]{1,0:T(8,128)(2,1)S(1)} %copy-done.4, f32[1,256,2048]{2,1,0:T(8,128)} %reduce-scatter.2.cloned.1.call-done, bf16[256,2048]{1,0:T(8,128)(2,1)S(1)} %copy-done.3, bf16[2048,2816]{1,0:T(8,128)(2,1)} %param.18, f32[256,2816]{1,0:T(8,128)} %fusion.21), kind=kOutput, calls=%fused_computation.6 | convolution fusion | flops 5912002560 | bytes 31195136 | tf_op jit(solution)/shard_map/dot_general | solution.py:24
  434.1 0.0 copy-done.1
  (4 shorter events, 0.1 us)
Async XLA Ops:
  6.5 3.9 copy-start
  6.6 45.5 %all-gather.6.cloned.1.call-start = ((), (), s32[]{:S(2)}) async-start(), calls=%async_computation.3 | async-start | bytes 1114112 | tf_op jit(solution)/shard_map/all_gather | solution.py:98
  10.4 1.3 copy-start.2
  11.6 132.6 %all-gather.4.cloned.1.call-start = ((), (), s32[]{:S(2)}) async-start(), calls=%async_computation.1 | async-start | bytes 17825792 | tf_op jit(solution)/shard_map/all_gather | solution.py:99
  12.5 405.4 %reduce-scatter.2.cloned.1.call-start = ((), (), s32[]{:S(2)}) async-start(), calls=%async_computation.2 | async-start | bytes 35651584 | tf_op jit(solution)/shard_map/reduce_scatter | solution.py:144
  238.6 1.2 copy-start.3
  239.8 178.1 %copy-start.4 = (bf16[256,2048]{1,0:T(8,128)(2,1)S(1)}, bf16[256,2048]{1,0:T(8,128)(2,1)}, u32[]{:S(2)}) copy-start(bf16[256,2048]{1,0:T(8,128)(2,1)} %param.10) | copy-start | bytes 3145732
  417.9 16.2 %copy-start.1 = (bf16[2048,64]{0,1:T(8,128)(2,1)S(1)}, bf16[2048,64]{0,1:T(8,128)(2,1)}, u32[]{:S(2)}) copy-start(bf16[2048,64]{0,1:T(8,128)(2,1)} %param.12) | copy-start | bytes 786436
Sparse Core Ops, SparseCore 0:
  11.8 40.2 all-gather.5
  53.7 90.4 all-gather.3
  238.7 179.0 reduce-scatter.1
